TPU v7x, 32 devices: a whole 2x2x4 slice. The times are simulated.
32 devices in a mesh: groups: 2 (over y), ctx: 4 (over z), head: 4 (over x, core).
Axes of the slice: x: 2, y: 2, z: 4, core: 2. Of those that a mesh axis runs over, the one named last changes fastest.
Arguments:
- query: bfloat16 [8, 64, 32, 128], P('groups', 'head'), parts along dimension 0
- key_cache: bfloat16 [8, 8192, 8, 128], P('groups', 'ctx', 'head'), parts along dimension 0
- value_cache: bfloat16 [8, 8192, 8, 128], P('groups', 'ctx', 'head'), parts along dimension 0, may hold values from -6 to 6
- new_key: bfloat16 [8, 8, 32, 128], P('groups', 'head'), parts along dimension 0, may hold values from -9 to 9
- new_value: bfloat16 [8, 8, 32, 128], P('groups', 'head'), parts along dimension 0, may hold values from -6 to 6
- lengths: int32 [8], P('groups'), parts along dimension 0, may hold values from 256 to 8192, as said below
- out_weight: bfloat16 [8192, 8192], P('head', 'ctx'), may hold values from -0.0625 to 0.0625
Outputs:
- projected: float32 [8, 32, 8192], P('groups', None, 'ctx'), parts along dimension 0
There are 2 independent parts, one for each index of `groups`. A program takes and returns all parts, laid end to end along the dimension named above; an argument that names none is the same for every part. Nothing has to cross between parts.
Inputs may be any that keep to these rules, and one draw needn't show every extreme that they name: `lengths`: multiples of 256; in every draw exactly one sequence has length 8192, the others less.
All inputs are finite; a program needn't handle non-finite values.
Results may differ from a plain program's by a relative error of at most 0.003.
Values sent between devices are 32-bit elements; how exact they have to be, the bound alone decides.
A program may use at most 128 MiB of HBM per device.

v0:
```python
import math

import jax
import jax.numpy as jnp
from jax import lax
from jax.sharding import PartitionSpec as P

very_low = -1e30


def shards(query, key_cache, value_cache, new_key, new_value, lengths, out_weight):
    seq_count, q_count, draft_len, head_dim = query.shape
    ctx_len = key_cache.shape[1]
    kv_count = key_cache.shape[2]
    group_rows = q_count // kv_count * draft_len
    scaling = 1.0 / math.sqrt(head_dim)
    grouped = query.reshape(seq_count, kv_count, group_rows, head_dim)
    scores = (
        jnp.einsum("sgrd,stgd->sgrt", grouped, key_cache, preferred_element_type=jnp.float32)
        * scaling
    )
    position = lax.axis_index("ctx") * ctx_len + jnp.arange(ctx_len, dtype=jnp.int32)
    usable = (position[None, :] < lengths[:, None])[:, None, None, :]
    masked = jnp.where(usable, scores, very_low)
    block_top = jnp.max(masked, axis=-1)
    weights = jnp.where(usable, jnp.exp(masked - block_top[..., None]), 0.0).astype(jnp.bfloat16)
    totals = jnp.sum(weights.astype(jnp.float32), axis=-1)
    numerators = jnp.einsum(
        "sgrt,stgd->sgrd", weights, value_cache, preferred_element_type=jnp.float32
    )
    global_top = lax.pmax(block_top, "ctx")
    factor = jnp.exp(block_top - global_top)
    totals, numerators = lax.psum((totals * factor, numerators * factor[..., None]), "ctx")
    own_scores = (
        jnp.einsum("sgrd,sgjd->sgrj", grouped, new_key, preferred_element_type=jnp.float32)
        * scaling
    )
    row_index = jnp.arange(group_rows) % draft_len
    causal = jnp.arange(draft_len)[None, :] <= row_index[:, None]
    own_scores = jnp.where(causal, own_scores, very_low)
    overall = jnp.maximum(global_top, jnp.max(own_scores, axis=-1))
    carried = jnp.exp(global_top - overall)
    fresh_weights = jnp.where(causal, jnp.exp(own_scores - overall[..., None]), 0.0)
    denominator = totals * carried + jnp.sum(fresh_weights, axis=-1)
    numerators = numerators * carried[..., None] + jnp.einsum(
        "sgrj,sgjd->sgrd", fresh_weights, new_value.astype(jnp.float32)
    )
    attended = (numerators / denominator[..., None]).reshape(
        seq_count, q_count, draft_len, head_dim
    )
    attended = (
        jnp.transpose(attended, (0, 2, 1, 3))
        .reshape(seq_count * draft_len, q_count * head_dim)
        .astype(jnp.bfloat16)
    )
    partial_out = jnp.dot(attended, out_weight, preferred_element_type=jnp.float32).reshape(
        seq_count, draft_len, -1
    )
    return lax.psum(partial_out, "head")


def solution(mesh):
    placed = (
        P("groups", "head", None, None),
        P("groups", "ctx", "head", None),
        P("groups", "ctx", "head", None),
        P("groups", "head", None, None),
        P("groups", "head", None, None),
        P("groups"),
        P("head", "ctx"),
    )
    return jax.shard_map(
        shards, mesh=mesh, in_specs=placed, out_specs=P("groups", None, "ctx"), check_vma=False
    )
```

profile of v0, /device:TPU:0, one launch (start us, length us, event | category | flops | bytes accessed | tf_op | source)
XLA Modules:
  0.0 152.1 jit_solution(4385293085769664509)
XLA Ops:
  6.5 0.0 copy-start
  6.5 0.0 all-reduce.3.cloned.1.call-start
  6.6 0.8 broadcast_compare_fusion
  7.4 0.2 copy-done
  7.6 0.0 copy-start.2
  7.6 9.6 %fusion = (f32[4,2,256]{2,1,0:T(2,128)S(1)}, f32[4,2,256,2048]{3,2,1,0:T(8,128)}) fusion(pred[4,2048]{1,0:T(4,128)(4,1)S(1)} %broadcast_compare_fusion, bf16[4,2,256,128]{3,2,1,0:T(8,128)(2,1)S(1)} %bitcast.28, bf16[4,2048,2,128]{3,2,1,0:T(2,128)(2,1)} %param.8), kind=kOutput, calls=%fused_computation.3 | convolution fusion | flops 1086322688 | bytes 21512192 | tf_op jit(solution)/shard_map/sgrd,stgd->sgrt/dot_general | solution.py:19
  17.2 13.7 %pmax.7 = f32[4,2,256]{2,1,0:T(2,128)S(1)} all-reduce(f32[4,2,256]{2,1,0:T(2,128)S(1)} %get-tuple-element.10), channel_id=1, replica_groups=mesh['groups'=2,'ctx'=4,'head'=4] {'ctx'}, use_global_device_ids=true, to_apply=%region_1.2 | all-reduce | flops 2048 | bytes 16384 | tf_op jit(solution)/shard_map/pmax | solution.py:31
  30.9 0.0 copy-start.1
  31.0 9.2 %convert_reduce_fusion = f32[4,2,256]{2,1,0:T(2,128)S(1)} fusion(f32[4,2,256]{2,1,0:T(2,128)S(1)} %get-tuple-element.10, f32[4,2,256,2048]{3,2,1,0:T(8,128)} %get-tuple-element.11, pred[4,2048]{1,0:T(4,128)(4,1)S(1)} %broadcast_compare_fusion), kind=kLoop, calls=%fused_computation | loop fusion | flops 29358080 | bytes 16801792 | tf_op jit(solution)/shard_map/reduce_sum | solution.py:27
  40.2 0.0 copy-done.2
  40.2 0.3 fusion.21
  40.5 1.1 copy-done.1
  41.6 0.0 copy-start.3
  41.6 7.5 %fusion.8 = f32[4,2,256,128]{3,2,1,0:T(8,128)} fusion(bf16[4,2048,2,128]{3,2,1,0:T(2,128)(2,1)} %param.9, f32[4,2,256]{2,1,0:T(2,128)S(1)} %bitcast.41, f32[4,2,256,2048]{3,2,1,0:T(8,128)S(1)} %copy-done.1, f32[4,2,256]{2,1,0:T(2,128)S(1)} %get-tuple-element.10, pred[4,2048]{1,0:T(4,128)(4,1)S(1)} %broadcast_compare_fusion), kind=kOutput, calls=%fused_computation.12 | convolution fusion | flops 1094975488 | bytes 22044672 | tf_op jit(solution)/shard_map/sgrt,stgd->sgrd/dot_general | solution.py:28
  49.1 0.0 all-reduce.3.cloned.1.call-update
  49.1 0.0 all-reduce.5.cloned.1.call-start
  49.2 8.5 %psum.22 = f32[4,2,256]{2,1,0:T(2,128)S(1)} all-reduce(f32[4,2,256]{2,1,0:T(2,128)S(1)} %bitcast.38), channel_id=1, replica_groups=mesh['groups'=2,'ctx'=4,'head'=4] {'ctx'}, use_global_device_ids=true, to_apply=%region_5.6 | all-reduce | flops 2048 | bytes 16384 | tf_op jit(solution)/shard_map/psum | solution.py:33
  57.7 0.1 fusion.15
  57.8 41.7 %all-reduce.3.cloned.1.call-done = f32[4,2,256,128]{3,2,1,0:T(8,128)} async-done(((f32[4,2,256,128]{3,2,1,0:T(8,128)}), f32[4,2,256,128]{3,2,1,0:T(8,128)}) %all-reduce.3.cloned.1.call-update) | async-done | bytes 1048592 | tf_op jit(solution)/shard_map/psum | solution.py:33
  99.5 0.0 copy-done.3
  99.5 2.0 %fusion.11 = bf16[4,2,256,128]{3,2,1,0:T(8,128)(2,1)S(1)} fusion(bf16[4,2,32,128]{3,2,1,0:T(8,128)(2,1)S(1)} %copy-done.3, f32[4,2,256,128]{3,2,1,0:T(8,128)} %all-reduce.3.cloned.1.call-done, f32[4,2,256]{2,1,0:T(2,128)S(1)} %bitcast.42, f32[4,2,256]{2,1,0:T(2,128)S(1)} %bitcast.43, f32[4,2,256,32]{2,3,1,0:T(8,128)S(1)} %get-tuple-element.13, ...), kind=kOutput, calls=%fused_computation.13 | convolution fusion | flops 17956864 | bytes 1933312 | tf_op jit(solution)/shard_map/sgrj,sgjd->sgrd/dot_general | solution.py:45
  101.5 5.7 %fusion.1 = f32[4,32,2048]{2,1,0:T(8,128)} fusion(bf16[2048,2048]{1,0:T(8,128)(2,1)} %param.13, bf16[4,16,4,8,128]{4,3,2,1,0:T(8,128)(2,1)S(1)} %bitcast.30), kind=kOutput, calls=%fused_computation.4 | convolution fusion | flops 1073741824 | bytes 9961472 | tf_op jit(solution)/shard_map/dot_general | solution.py:56
  107.2 0.0 all-reduce.5.cloned.1.call-update
  107.3 35.7 %all-reduce.5.cloned.1.call-done = f32[4,32,2048]{2,1,0:T(8,128)} async-done(((f32[4,32,2048]{2,1,0:T(8,128)}), f32[4,32,2048]{2,1,0:T(8,128)}) %all-reduce.5.cloned.1.call-update) | async-done | bytes 1048592 | tf_op jit(solution)/shard_map/psum | solution.py:59
  143.0 2.3 %copy.26 = f32[4,32,2048]{2,1,0:T(8,128)} copy(f32[4,32,2048]{2,1,0:T(8,128)} %all-reduce.5.cloned.1.call-done) | data formatting | bytes 2097152
  (5 shorter events, 0.0 us)
Async XLA Ops:
  6.5 1.1 copy-start
  6.5 93.0 %all-reduce.3.cloned.1.call-start = ((), (), s32[]{:S(2)}) async-start(), calls=%async_computation | async-start | bytes 2097152 | tf_op jit(solution)/shard_map/psum | solution.py:33
  7.6 32.6 %copy-start.2 = (bf16[4,2,32,128]{3,2,1,0:T(8,128)(2,1)S(1)}, bf16[4,2,32,128]{3,2,1,0:T(8,128)(2,1)}, u32[]{:S(2)}) copy-start(bf16[4,2,32,128]{3,2,1,0:T(8,128)(2,1)} %param.10) | copy-start | bytes 196612
  30.9 10.7 %copy-start.1 = (f32[4,2,256,2048]{3,2,1,0:T(8,128)S(1)}, f32[4,2,256,2048]{3,2,1,0:T(8,128)}, u32[]{:S(2)}) copy-start(f32[4,2,256,2048]{3,2,1,0:T(8,128)} %get-tuple-element.11) | copy-start | bytes 50331652
  41.6 57.9 %copy-start.3 = (bf16[4,2,32,128]{3,2,1,0:T(8,128)(2,1)S(1)}, bf16[4,2,32,128]{3,2,1,0:T(8,128)(2,1)}, u32[]{:S(2)}) copy-start(bf16[4,2,32,128]{3,2,1,0:T(8,128)(2,1)} %param.11) | copy-start | bytes 196612
  49.1 93.8 %all-reduce.5.cloned.1.call-start = ((), (), s32[]{:S(2)}) async-start(), calls=%async_computation.1 | async-start | bytes 2097152 | tf_op jit(solution)/shard_map/psum | solution.py:59
Sparse Core Ops, SparseCore 0:
  49.3 50.1 all-reduce.2
  107.4 35.5 all-reduce.4
where the time goes:
time: 152 us
  waiting for transfers between devices  77.4 us (51%)
  matrix products  25.1 us (17%)
  blocking collectives  22.2 us (15%)
  between operations  13.5 us (9%)
  other arithmetic  10.1 us (7%)
  local copies, waits for them, and re-layouts  3.66 us (2%)
    psum x1, waiting for transfers between devices, shards(): lax.psum((totals * factor, numerators * factor[..., None]), 'ctx')  41.7 us
    psum x1, waiting for transfers between devices, shards(): return lax.psum(partial_out, 'head')  35.7 us
    pmax x1, blocking collectives, shards(): global_top = lax.pmax(block_top, 'ctx')  13.7 us
    dot_general x1, matrix products, shards(): jnp.einsum('sgrd,stgd->sgrt', grouped, key_cache, preferred_element_type=...  9.62 us
    reduce_sum x1, other arithmetic, shards(): totals = jnp.sum(weights.astype(jnp.float32), axis=-1)  9.21 us
    psum x1, blocking collectives, shards(): lax.psum((totals * factor, numerators * factor[..., None]), 'ctx')  8.53 us
    dot_general x1, matrix products, shards(): jnp.einsum('sgrt,stgd->sgrd', weights, value_cache, preferred_element_typ...  7.5 us
    dot_general x1, matrix products, shards(): jnp.dot(attended, out_weight, preferred_element_type=jnp.float32)  5.71 us
  transfers between devices with their start and end apart: 2, of which 2 were waited for; matrix products, arithmetic and copies ran while one was open for 0% of the time, Pallas kernels for 0%

commit v1 on v0

--- a/solution.py
+++ b/solution.py
@@ -1,14 +1,20 @@
+import functools
 import math
 
 import jax
 import jax.numpy as jnp
 from jax import lax
+from jax.experimental import pallas as pl
+from jax.experimental.pallas import tpu as pltpu
 from jax.sharding import PartitionSpec as P
 
 very_low = -1e30
-
-
-def shards(query, key_cache, value_cache, new_key, new_value, lengths, out_weight):
+MESH = pl.DeviceIdType.MESH
+LANES = 128
+PAGE = 256
+
+
+def plain_shards(query, key_cache, value_cache, new_key, new_value, lengths, out_weight):
     seq_count, q_count, draft_len, head_dim = query.shape
     ctx_len = key_cache.shape[1]
     kv_count = key_cache.shape[2]
@@ -59,6 +65,321 @@
     return lax.psum(partial_out, "head")
 
 
+def column(values, at):
+    return values[:, at : at + 1]
+
+
+def kernel(
+    n, draft, chunk,
+    q_ref, k_hbm, v_hbm, nk_ref, nv_ref, len_ref, w_hbm, out_ref,
+    kbuf, vbuf, wbuf, sbuf, acc, msg, rmsg, ag, send_a, keep, recv_a, send_b, recv_b,
+    ksem, vsem, wsem, rs_send, rs_recv, ag_send, ag_recv,
+    a_send, a_recv, b_send, b_recv, c_send, c_recv,
+):
+    me = lax.axis_index("ctx")
+    head = lax.axis_index("head")
+    side = lax.rem(head, 2)
+    other = 1 - side
+    pair = head - side + other
+    upper = lax.rem(lax.div(head, 2), 2)
+    across = head + 2 - 4 * upper
+    rows = q_ref.shape[1] // 2
+    span = kbuf.shape[1]
+    half = wbuf.shape[2]
+    steps = span // chunk
+    scale = math.log2(math.e) / math.sqrt(q_ref.shape[2])
+    order = [k for k in (1, n - 1) + tuple(range(2, n - 1))]
+
+    def seq_at(offset):
+        return lax.rem(me + offset, n)
+
+    barrier = pltpu.get_barrier_semaphore()
+    for offset in range(1, n):
+        pl.semaphore_signal(barrier, inc=1, device_id={"ctx": seq_at(offset)}, device_id_type=MESH)
+    pl.semaphore_signal(barrier, inc=1, device_id={"head": pair}, device_id_type=MESH)
+    pl.semaphore_signal(barrier, inc=1, device_id={"head": across}, device_id_type=MESH)
+
+    def k_copy(offset):
+        s = seq_at(offset)
+        return pltpu.make_async_copy(k_hbm.at[s], kbuf.at[offset], ksem.at[offset])
+
+    def v_copy(offset):
+        s = seq_at(offset)
+        return pltpu.make_async_copy(v_hbm.at[s], vbuf.at[offset], vsem.at[offset])
+
+    def w_copy(i):
+        return pltpu.make_async_copy(w_hbm.at[:, pl.ds(i * half, half)], wbuf.at[i], wsem.at[i])
+
+    for offset in order + [0]:
+        k_copy(offset).start()
+        v_copy(offset).start()
+    w_copy(0).start()
+    w_copy(1).start()
+
+    lane = lax.broadcasted_iota(jnp.int32, (rows, LANES), 1)
+    even_lane = lax.rem(lane, 2) == 0
+    sub = lax.broadcasted_iota(jnp.int32, (1, 16, LANES), 1)
+    even_row = jnp.where(lax.rem(sub, 2) == 0, 1.0, 0.0).astype(jnp.bfloat16)
+    odd_row = jnp.where(lax.rem(sub, 2) == 0, 0.0, 1.0).astype(jnp.bfloat16)
+
+    def spread(block):
+        tiles = block.reshape(chunk // 16, 16, LANES)
+        return jnp.concatenate(
+            [(tiles * even_row).reshape(chunk, LANES), (tiles * odd_row).reshape(chunk, LANES)],
+            axis=1,
+        )
+
+    def attend(offset):
+        s = seq_at(offset)
+        grouped = jnp.concatenate([q_ref[s, :rows], q_ref[s, rows:]], axis=1)
+        usable = len_ref[s] - me * (span // 2)
+        k_copy(offset).wait()
+        per = 2 * PAGE
+
+        def bias(j, page):
+            return jnp.where((j * (chunk // per) + page) * PAGE < usable, 0.0, -very_low)
+
+        def score(j, top):
+            at = pl.multiple_of(j * chunk, chunk)
+            keys = spread(kbuf[offset, pl.ds(at, chunk), :])
+            scores = lax.dot_general(
+                grouped, keys, (((1,), (1,)), ((), ())), preferred_element_type=jnp.float32
+            )
+            sbuf[j] = scores
+            for page in range(chunk // per):
+                tiles = [
+                    scores[:, page * per + i * LANES : page * per + (i + 1) * LANES]
+                    for i in range(per // LANES)
+                ]
+                top = jnp.maximum(top, functools.reduce(jnp.maximum, tiles) - bias(j, page))
+            return top
+
+        top = lax.fori_loop(0, steps, score, jnp.full((rows, LANES), very_low, jnp.float32))
+        tops = [
+            jnp.max(jnp.where(even_lane, top, very_low), axis=1, keepdims=True) * scale,
+            jnp.max(jnp.where(even_lane, very_low, top), axis=1, keepdims=True) * scale,
+        ]
+        shift = jnp.where(even_lane, tops[0], tops[1])
+        v_copy(offset).wait()
+        acc[...] = jnp.zeros_like(acc)
+
+        def weigh(j, total):
+            at = pl.multiple_of(j * chunk, chunk)
+            pieces = []
+            for page in range(chunk // per):
+                shifted = shift + bias(j, page)
+                for i in range(per // LANES):
+                    piece = jnp.exp2(
+                        sbuf[j, :, page * per + i * LANES : page * per + (i + 1) * LANES] * scale
+                        - shifted
+                    )
+                    total = total + piece
+                    pieces.append(piece.astype(jnp.bfloat16))
+            weights = jnp.concatenate(pieces, axis=1)
+            values = spread(vbuf[offset, pl.ds(at, chunk), :])
+            acc[...] += jnp.dot(weights, values, preferred_element_type=jnp.float32)
+            return total
+
+        total = lax.fori_loop(0, steps, weigh, jnp.zeros((rows, LANES), jnp.float32))
+        sums = [
+            jnp.sum(jnp.where(even_lane, total, 0.0), axis=1, keepdims=True),
+            jnp.sum(jnp.where(even_lane, 0.0, total), axis=1, keepdims=True),
+        ]
+        return tops, sums
+
+    def send_partial(offset):
+        return pltpu.make_async_remote_copy(
+            src_ref=msg.at[offset - 1], dst_ref=rmsg.at[offset - 1],
+            send_sem=rs_send.at[offset - 1], recv_sem=rs_recv.at[offset - 1],
+            device_id={"ctx": seq_at(offset)}, device_id_type=MESH,
+        )
+
+    for index, offset in enumerate(order):
+        tops, sums = attend(offset)
+        slot = offset - 1
+        msg[slot, :rows, :] = acc[:, :LANES]
+        msg[slot, rows : 2 * rows, :] = acc[:, LANES:]
+        stats = jnp.where(
+            lane == 0, tops[0],
+            jnp.where(lane == 1, sums[0], jnp.where(lane == 2, tops[1], sums[1])),
+        ).T
+        for i in range(rows // LANES):
+            msg[slot, 2 * rows + 8 * i : 2 * rows + 8 * (i + 1), :] = stats[
+                :8, i * LANES : (i + 1) * LANES
+            ]
+        if index == 0:
+            pl.semaphore_wait(barrier, n + 1)
+        send_partial(offset).start()
+
+    tops, sums = attend(0)
+    row_in = lax.rem(lax.broadcasted_iota(jnp.int32, (rows, draft), 0), draft)
+    causal = lax.broadcasted_iota(jnp.int32, (rows, draft), 1) <= row_in
+    own = []
+    for g in range(2):
+        fresh = lax.dot_general(
+            q_ref[me, g * rows : (g + 1) * rows], nk_ref[me, g],
+            (((1,), (1,)), ((), ())), preferred_element_type=jnp.float32,
+        ) * scale
+        fresh = jnp.where(causal, fresh, very_low)
+        own.append((fresh, jnp.max(fresh, axis=1, keepdims=True)))
+
+    stats = []
+    for offset in order:
+        send_partial(offset).wait_recv()
+        slot = offset - 1
+        packed = jnp.concatenate(
+            [rmsg[slot, 2 * rows + 8 * i : 2 * rows + 8 * (i + 1), :] for i in range(rows // LANES)],
+            axis=1,
+        )
+        packed = jnp.concatenate([packed, jnp.zeros((LANES - 8, rows), jnp.float32)], axis=0)
+        stats.append((slot, packed.T))
+
+    for g in range(2):
+        fresh, fresh_top = own[g]
+        overall = jnp.maximum(tops[g], fresh_top)
+        for slot, values in stats:
+            overall = jnp.maximum(overall, column(values, 2 * g))
+        fresh = jnp.where(causal, jnp.exp2(fresh - overall), 0.0)
+        carried = jnp.exp2(tops[g] - overall)
+        denominator = jnp.sum(fresh, axis=1, keepdims=True) + sums[g] * carried
+        numerator = acc[:, g * LANES : (g + 1) * LANES] * carried + jnp.dot(
+            fresh.astype(jnp.bfloat16), nv_ref[me, g], preferred_element_type=jnp.float32
+        )
+        for slot, values in stats:
+            carried = jnp.exp2(column(values, 2 * g) - overall)
+            denominator = denominator + column(values, 2 * g + 1) * carried
+            numerator = numerator + rmsg[slot, g * rows : (g + 1) * rows, :] * carried
+        ag[0, g * rows : (g + 1) * rows, :] = numerator / denominator
+
+    def send_attended(offset):
+        return pltpu.make_async_remote_copy(
+            src_ref=ag.at[0], dst_ref=ag.at[offset],
+            send_sem=ag_send.at[offset - 1], recv_sem=ag_recv.at[offset - 1],
+            device_id={"ctx": seq_at(offset)}, device_id_type=MESH,
+        )
+
+    for offset in order:
+        send_attended(offset).start()
+
+    def swap_a(slot):
+        return pltpu.make_async_remote_copy(
+            src_ref=send_a.at[slot], dst_ref=recv_a.at[slot],
+            send_sem=a_send.at[slot], recv_sem=a_recv.at[slot],
+            device_id={"head": pair}, device_id_type=MESH,
+        )
+
+    def swap_b(slot):
+        return pltpu.make_async_remote_copy(
+            src_ref=send_b.at[slot], dst_ref=recv_b.at[slot],
+            send_sem=b_send.at[slot], recv_sem=b_recv.at[slot],
+            device_id={"head": across}, device_id_type=MESH,
+        )
+
+    def swap_c(slot):
+        s = seq_at(n - slot)
+        return pltpu.make_async_remote_copy(
+            src_ref=out_ref.at[side, s], dst_ref=out_ref.at[side, s],
+            send_sem=c_send.at[slot], recv_sem=c_recv.at[slot],
+            device_id={"head": pair}, device_id_type=MESH,
+        )
+
+    wide = 2 * LANES
+
+    def project(slot):
+        heads = ag.shape[1] // draft
+        attended = jnp.concatenate(
+            [ag[slot, h * draft : (h + 1) * draft, :].astype(jnp.bfloat16) for h in range(heads)],
+            axis=1,
+        )
+        for target, which in ((send_a, other), (keep, side)):
+            @pl.loop(0, half // wide)
+            def _(i):
+                at = pl.ds(pl.multiple_of(i * wide, wide), wide)
+                target[slot, :, at] = jnp.dot(
+                    attended, wbuf[which, :, at], preferred_element_type=jnp.float32
+                )
+            if target is send_a:
+                swap_a(slot).start()
+
+    def join_pair(slot):
+        swap_a(slot).wait_recv()
+        send_b[slot] = keep[slot] + recv_a[slot]
+        swap_b(slot).start()
+
+    def join_across(slot):
+        swap_b(slot).wait_recv()
+        out_ref[side, seq_at(n - slot)] = send_b[slot] + recv_b[slot]
+        swap_c(slot).start()
+
+    w_copy(0).wait()
+    w_copy(1).wait()
+    slots = [0] + order
+    for i in range(n + 2):
+        if i < n:
+            if slots[i]:
+                send_attended(slots[i]).wait_recv()
+            project(slots[i])
+        if 0 <= i - 1 < n:
+            join_pair(slots[i - 1])
+        if 0 <= i - 2:
+            join_across(slots[i - 2])
+
+    for slot in slots:
+        swap_c(slot).wait_recv()
+        swap_a(slot).wait_send()
+        swap_b(slot).wait_send()
+        swap_c(slot).wait_send()
+        if slot:
+            send_partial(slot).wait_send()
+            send_attended(slot).wait_send()
+
+
+def shards(n, query, key_cache, value_cache, new_key, new_value, lengths, out_weight):
+    seqs, q_count, draft, dim = query.shape
+    ctx_len, kv_count = key_cache.shape[1:3]
+    rows = q_count // 2 * draft
+    features, width = out_weight.shape
+    span = 2 * ctx_len
+    chunk = 4 * PAGE
+    half = width // 2
+    f32 = jnp.float32
+    vmem = pl.BlockSpec(memory_space=pltpu.VMEM)
+    anywhere = pl.BlockSpec(memory_space=pl.ANY)
+    dma = pltpu.SemaphoreType.DMA
+    out = pl.pallas_call(
+        functools.partial(kernel, n, draft, chunk),
+        out_shape=jax.ShapeDtypeStruct((2, seqs, draft, half), f32),
+        in_specs=[
+            vmem, anywhere, anywhere, vmem, vmem,
+            pl.BlockSpec(memory_space=pltpu.SMEM), anywhere,
+        ],
+        out_specs=vmem,
+        scratch_shapes=[
+            pltpu.VMEM((n, span, dim), key_cache.dtype),
+            pltpu.VMEM((n, span, dim), value_cache.dtype),
+            pltpu.VMEM((2, features, half), out_weight.dtype),
+            pltpu.VMEM((span // chunk, rows, chunk), f32),
+            pltpu.VMEM((rows, 2 * dim), f32),
+            pltpu.VMEM((n - 1, 2 * rows + 8 * (rows // LANES), dim), f32),
+            pltpu.VMEM((n - 1, 2 * rows + 8 * (rows // LANES), dim), f32),
+            pltpu.VMEM((n, 2 * rows, dim), f32),
+        ]
+        + [pltpu.VMEM((n, draft, half), f32)] * 5
+        + [dma((n,)), dma((n,)), dma((2,))]
+        + [dma((n - 1,))] * 4
+        + [dma((n,))] * 6,
+        compiler_params=pltpu.CompilerParams(
+            collective_id=0, has_side_effects=True, vmem_limit_bytes=56 * 2**20
+        ),
+    )(
+        query.reshape(seqs, q_count * draft, dim),
+        key_cache.reshape(seqs, span, dim),
+        value_cache.reshape(seqs, span, dim),
+        new_key, new_value, lengths, out_weight,
+    )
+    return jnp.transpose(out, (1, 2, 0, 3)).reshape(seqs, draft, width)
+
+
 def solution(mesh):
     placed = (
         P("groups", "head", None, None),
@@ -69,6 +390,21 @@
         P("groups"),
         P("head", "ctx"),
     )
+    ctx, heads = mesh.shape["ctx"], mesh.shape["head"]
+
+    def body(query, key_cache, *rest):
+        fits = (
+            query.shape[0] == ctx
+            and ctx >= 3
+            and heads == 4
+            and key_cache.shape[2] == 2
+            and query.shape[3] == LANES
+            and key_cache.shape[1] % (2 * PAGE) == 0
+        )
+        if fits:
+            return shards(ctx, query, key_cache, *rest)
+        return plain_shards(query, key_cache, *rest)
+
     return jax.shard_map(
-        shards, mesh=mesh, in_specs=placed, out_specs=P("groups", None, "ctx"), check_vma=False
-    )
+        body, mesh=mesh, in_specs=placed, out_specs=P("groups", None, "ctx"), check_vma=False
+    )

time: 152 us -> 72.3 us (0.48)
  waiting for transfers between devices: 77.4 us -> 0 us
  Pallas kernels: 0 us -> 69.8 us
  matrix products: 25.1 us -> 0 us
  blocking collectives: 22.2 us -> 0 us
  between operations: 13.5 us -> 0.01 us
  other arithmetic: 10.1 us -> 0 us
    psum x2 -> x0, waiting for transfers between devices: 77.4 us -> none  [the longest x1 41.7 us: shards(): lax.psum((totals * factor, numerators * factor[..., None]), 'ctx')]
    pallas_call x0 -> x1, Pallas kernels: none -> 69.8 us  [shards(): pl.pallas_call(functools.partial(kernel, n, draft, chunk), out_shape=jax....]
    dot_general x5 -> x0, matrix products: 25.1 us -> none  [the longest x1 9.62 us: shards(): jnp.einsum('sgrd,stgd->sgrt', grouped, key_cache, preferred_element_type=...]
    pmax x1 -> x0, blocking collectives: 13.7 us -> none  [shards(): global_top = lax.pmax(block_top, 'ctx')]
    reduce_sum x2 -> x0, other arithmetic: 9.29 us -> none  [the longest x1 9.21 us: shards(): totals = jnp.sum(weights.astype(jnp.float32), axis=-1)]
    psum x1 -> x0, blocking collectives: 8.53 us -> none  [shards(): lax.psum((totals * factor, numerators * factor[..., None]), 'ctx')]
    unnamed x9 -> x0, local copies, waits for them, and re-layouts: 3.66 us -> none
    reshape x0 -> x1, local copies, waits for them, and re-layouts: none -> 2.31 us  [shards(): return jnp.transpose(out, (1, 2, 0, 3)).reshape(seqs, draft, width)]
  transfers between devices with their start and end apart: 2 -> 0, of which waited for: 2 -> 0; matrix products, arithmetic and copies ran while one was open for 0% -> 0% of each run, Pallas kernels for 0% -> 0%
where the time goes in v1:
time: 72.3 us; the launch traced here: 72.1 us
  Pallas kernels  69.8 us (97%)
  local copies, waits for them, and re-layouts  2.31 us (3%)
    pallas_call x1, Pallas kernels, shards(): pl.pallas_call(functools.partial(kernel, n, draft, chunk), out_shape=jax....  69.8 us
    reshape x1, local copies, waits for them, and re-layouts, shards(): return jnp.transpose(out, (1, 2, 0, 3)).reshape(seqs, draft, width)  2.31 us

profile of v1, /device:TPU:0, one launch (start us, length us, event | category | flops | bytes accessed | tf_op | source)
XLA Modules:
  0.0 72.1 jit_solution(7568325006434107359)
XLA Ops:
  0.0 69.8 %shard_map.73 = f32[2,4,32,1024]{3,2,1,0:T(8,128)} custom-call(bf16[4,512,128]{2,1,0:T(8,128)(2,1)} %bitcast.9, bf16[4,4096,128]{2,1,0:T(8,128)(2,1)} %bitcast.6, bf16[4,4096,128]{2,1,0:T(8,128)(2,1)} %bitcast.7, bf16[4,2,32,128]{3,2,1,0:T(8,128)(2,1)} %nk_ref.1, bf16[4,2,32,128]{3,2,1,0:T(8,128)(2,1)} %nv_ref.1, s32[4]{0:T(128)} %len_ref.1, ...), custom_call_target="tpu_custom_call" | custom-call | tf_op jit(solution)/shard_map/pallas_call | solution.py:349
  69.8 2.3 %copy.9 = f32[2,4,4,8,1024]{4,3,0,2,1:T(8,128)} copy(f32[2,4,4,8,1024]{4,3,2,1,0:T(8,128)} %bitcast.8) | data formatting | bytes 2097152 | tf_op jit(solution)/shard_map/reshape | solution.py:380

commit v2 on v1

v2 whole, which is shorter than its diff:
```python
import functools
import math

import jax
import jax.numpy as jnp
from jax import lax
from jax.experimental import pallas as pl
from jax.experimental.pallas import tpu as pltpu
from jax.sharding import PartitionSpec as P

very_low = -1e30
MESH = pl.DeviceIdType.MESH
LANES = 128
PAGE = 256


def plain_shards(query, key_cache, value_cache, new_key, new_value, lengths, out_weight):
    seq_count, q_count, draft_len, head_dim = query.shape
    ctx_len = key_cache.shape[1]
    kv_count = key_cache.shape[2]
    group_rows = q_count // kv_count * draft_len
    scaling = 1.0 / math.sqrt(head_dim)
    grouped = query.reshape(seq_count, kv_count, group_rows, head_dim)
    scores = (
        jnp.einsum("sgrd,stgd->sgrt", grouped, key_cache, preferred_element_type=jnp.float32)
        * scaling
    )
    position = lax.axis_index("ctx") * ctx_len + jnp.arange(ctx_len, dtype=jnp.int32)
    usable = (position[None, :] < lengths[:, None])[:, None, None, :]
    masked = jnp.where(usable, scores, very_low)
    block_top = jnp.max(masked, axis=-1)
    weights = jnp.where(usable, jnp.exp(masked - block_top[..., None]), 0.0).astype(jnp.bfloat16)
    totals = jnp.sum(weights.astype(jnp.float32), axis=-1)
    numerators = jnp.einsum(
        "sgrt,stgd->sgrd", weights, value_cache, preferred_element_type=jnp.float32
    )
    global_top = lax.pmax(block_top, "ctx")
    factor = jnp.exp(block_top - global_top)
    totals, numerators = lax.psum((totals * factor, numerators * factor[..., None]), "ctx")
    own_scores = (
        jnp.einsum("sgrd,sgjd->sgrj", grouped, new_key, preferred_element_type=jnp.float32)
        * scaling
    )
    row_index = jnp.arange(group_rows) % draft_len
    causal = jnp.arange(draft_len)[None, :] <= row_index[:, None]
    own_scores = jnp.where(causal, own_scores, very_low)
    overall = jnp.maximum(global_top, jnp.max(own_scores, axis=-1))
    carried = jnp.exp(global_top - overall)
    fresh_weights = jnp.where(causal, jnp.exp(own_scores - overall[..., None]), 0.0)
    denominator = totals * carried + jnp.sum(fresh_weights, axis=-1)
    numerators = numerators * carried[..., None] + jnp.einsum(
        "sgrj,sgjd->sgrd", fresh_weights, new_value.astype(jnp.float32)
    )
    attended = (numerators / denominator[..., None]).reshape(
        seq_count, q_count, draft_len, head_dim
    )
    attended = (
        jnp.transpose(attended, (0, 2, 1, 3))
        .reshape(seq_count * draft_len, q_count * head_dim)
        .astype(jnp.bfloat16)
    )
    partial_out = jnp.dot(attended, out_weight, preferred_element_type=jnp.float32).reshape(
        seq_count, draft_len, -1
    )
    return lax.psum(partial_out, "head")


def kernel(
    draft, chunk,
    q_ref, k_hbm, v_hbm, nk_ref, nv_ref, len_ref, w_hbm, out_ref,
    kbuf, vbuf, wbuf, sbuf, acc, msg, rmsg, mid, rmid, ag, send_a, keep, recv_a, send_b, recv_b,
    ksem, vsem, wsem, rs_send, rs_recv, mid_send, mid_recv, down_send, down_recv,
    over_send, over_recv, a_send, a_recv, b_send, b_recv, c_send, c_recv,
):
    me = lax.axis_index("ctx")
    head = lax.axis_index("head")
    side = lax.rem(head, 2)
    other = 1 - side
    pair = head - side + other
    upper = lax.rem(lax.div(head, 2), 2)
    across = head + 2 - 4 * upper
    low, high = lax.rem(me, 2), lax.div(me, 2)
    inner = low != high
    outer = low == high
    mate = me + 1 - 2 * low
    facing = 3 - me
    rows = q_ref.shape[1] // 2
    span = kbuf.shape[1]
    half = wbuf.shape[2]
    steps = span // chunk
    blocks = rows // LANES
    scale = math.log2(math.e) / math.sqrt(q_ref.shape[2])

    def seq_of(place):
        return 2 * (high if place % 2 else 1 - high) + place // 2

    barrier = pltpu.get_barrier_semaphore()
    for target in ({"ctx": mate}, {"ctx": facing}, {"head": pair}, {"head": across}):
        pl.semaphore_signal(barrier, inc=1, device_id=target, device_id_type=MESH)

    def k_copy(place):
        return pltpu.make_async_copy(k_hbm.at[seq_of(place)], kbuf.at[place], ksem.at[place])

    def v_copy(place):
        return pltpu.make_async_copy(v_hbm.at[seq_of(place)], vbuf.at[place], vsem.at[place])

    def w_copy(i):
        return pltpu.make_async_copy(w_hbm.at[:, pl.ds(i * half, half)], wbuf.at[i], wsem.at[i])

    for place in range(4):
        k_copy(place).start()
        v_copy(place).start()
    w_copy(0).start()
    w_copy(1).start()

    lane = lax.broadcasted_iota(jnp.int32, (rows, LANES), 1)
    even_lane = lax.rem(lane, 2) == 0
    sub = lax.broadcasted_iota(jnp.int32, (1, 16, LANES), 1)
    even_row = jnp.where(lax.rem(sub, 2) == 0, 1.0, 0.0).astype(jnp.bfloat16)
    odd_row = jnp.where(lax.rem(sub, 2) == 0, 0.0, 1.0).astype(jnp.bfloat16)

    def spread(block):
        tiles = block.reshape(chunk // 16, 16, LANES)
        return jnp.concatenate(
            [(tiles * even_row).reshape(chunk, LANES), (tiles * odd_row).reshape(chunk, LANES)],
            axis=1,
        )

    def pack(ref, top, total):
        stats = jnp.where(lane == 0, top, total).T
        for i in range(blocks):
            ref[rows + 8 * i : rows + 8 * (i + 1), :] = stats[:8, i * LANES : (i + 1) * LANES]

    def unpack(ref):
        packed = jnp.concatenate(
            [ref[rows + 8 * i : rows + 8 * (i + 1), :] for i in range(blocks)], axis=1
        )
        packed = jnp.concatenate([packed, jnp.zeros((LANES - 8, rows), jnp.float32)], axis=0).T
        return packed[:, 0:1], packed[:, 1:2]

    def attend(place):
        s = seq_of(place)
        grouped = jnp.concatenate([q_ref[s, :rows], q_ref[s, rows:]], axis=1)
        usable = len_ref[s] - me * (span // 2)
        k_copy(place).wait()
        per = 2 * PAGE

        def bias(j, page):
            return jnp.where((j * (chunk // per) + page) * PAGE < usable, 0.0, -very_low)

        def score(j, top):
            at = pl.multiple_of(j * chunk, chunk)
            keys = spread(kbuf[place, pl.ds(at, chunk), :])
            scores = lax.dot_general(
                grouped, keys, (((1,), (1,)), ((), ())), preferred_element_type=jnp.float32
            )
            sbuf[j] = scores
            for page in range(chunk // per):
                tiles = [
                    scores[:, page * per + i * LANES : page * per + (i + 1) * LANES]
                    for i in range(per // LANES)
                ]
                top = jnp.maximum(top, functools.reduce(jnp.maximum, tiles) - bias(j, page))
            return top

        top = lax.fori_loop(0, steps, score, jnp.full((rows, LANES), very_low, jnp.float32))
        tops = [
            jnp.max(jnp.where(even_lane, top, very_low), axis=1, keepdims=True) * scale,
            jnp.max(jnp.where(even_lane, very_low, top), axis=1, keepdims=True) * scale,
        ]
        shift = jnp.where(even_lane, tops[0], tops[1])
        v_copy(place).wait()
        acc[...] = jnp.zeros_like(acc)

        def weigh(j, total):
            at = pl.multiple_of(j * chunk, chunk)
            pieces = []
            for page in range(chunk // per):
                shifted = shift + bias(j, page)
                for i in range(per // LANES):
                    piece = jnp.exp2(
                        sbuf[j, :, page * per + i * LANES : page * per + (i + 1) * LANES] * scale
                        - shifted
                    )
                    total = total + piece
                    pieces.append(piece.astype(jnp.bfloat16))
            weights = jnp.concatenate(pieces, axis=1)
            values = spread(vbuf[place, pl.ds(at, chunk), :])
            acc[...] += jnp.dot(weights, values, preferred_element_type=jnp.float32)
            return total

        total = lax.fori_loop(0, steps, weigh, jnp.zeros((rows, LANES), jnp.float32))
        sums = [
            jnp.sum(jnp.where(even_lane, total, 0.0), axis=1, keepdims=True),
            jnp.sum(jnp.where(even_lane, 0.0, total), axis=1, keepdims=True),
        ]
        for g in range(2):
            ref = msg.at[place, g]
            ref[:rows, :] = acc[:, g * LANES : (g + 1) * LANES]
            pack(ref, tops[g], sums[g])

    def remote(source, target, send, recv, axis, device):
        return pltpu.make_async_remote_copy(
            src_ref=source, dst_ref=target, send_sem=send, recv_sem=recv,
            device_id={axis: device}, device_id_type=MESH,
        )

    def inward(p, g):
        return remote(
            msg.at[p, g], rmsg.at[p, g], rs_send.at[p, g], rs_recv.at[p, g], "ctx", mate
        )

    def through(i, g):
        return remote(
            mid.at[i, g], rmid.at[i, g], mid_send.at[i, g], mid_recv.at[i, g], "ctx", facing
        )

    def outward(p, g):
        return remote(
            ag.at[p, g], ag.at[p, g], down_send.at[p, g], down_recv.at[p, g], "ctx", mate
        )

    def over(i, g):
        return remote(
            ag.at[2 * i + 1, g], ag.at[2 * i, g],
            over_send.at[i, g], over_recv.at[i, g], "ctx", facing,
        )

    def join(parts, overall, total, numerator):
        for ref, (top, amount) in parts:
            carried = jnp.exp2(top - overall)
            total = total + amount * carried
            numerator = numerator + ref[:rows, :] * carried
        return total, numerator

    def send_inward(place):
        @pl.when(outer)
        def _():
            for g in range(2):
                inward(place, g).start()

    def merge(i):
        @pl.when(inner)
        def _():
            for g in range(2):
                inward(2 * i, g).wait_recv()
                parts = [(r, unpack(r)) for r in (msg.at[2 * i, g], rmsg.at[2 * i, g])]
                overall = jnp.maximum(parts[0][1][0], parts[1][1][0])
                total, numerator = join(parts, overall, 0.0, 0.0)
                mid[i, g, :rows, :] = numerator
                pack(mid.at[i, g], overall, total)
                through(i, g).start()

    row_in = lax.rem(lax.broadcasted_iota(jnp.int32, (rows, draft), 0), draft)
    causal = lax.broadcasted_iota(jnp.int32, (rows, draft), 1) <= row_in

    def finish(i):
        @pl.when(inner)
        def _():
            place = 2 * i + 1
            s = seq_of(place)
            for g in range(2):
                fresh = lax.dot_general(
                    q_ref[s, g * rows : (g + 1) * rows], nk_ref[s, g],
                    (((1,), (1,)), ((), ())), preferred_element_type=jnp.float32,
                ) * scale
                fresh = jnp.where(causal, fresh, very_low)
                overall = jnp.max(fresh, axis=1, keepdims=True)
                through(i, g).wait_recv()
                inward(place, g).wait_recv()
                refs = (msg.at[place, g], rmsg.at[place, g], rmid.at[i, g])
                parts = [(r, unpack(r)) for r in refs]
                for _, (top, _) in parts:
                    overall = jnp.maximum(overall, top)
                fresh = jnp.where(causal, jnp.exp2(fresh - overall), 0.0)
                total, numerator = join(
                    parts, overall,
                    jnp.sum(fresh, axis=1, keepdims=True),
                    jnp.dot(
                        fresh.astype(jnp.bfloat16), nv_ref[s, g],
                        preferred_element_type=jnp.float32,
                    ),
                )
                ag[place, g] = numerator / total
                over(i, g).start()
                outward(place, g).start()

    def arrive(place):
        @pl.when(outer)
        def _():
            for g in range(2):
                outward(place, g).wait_recv()

        if place % 2 == 0:
            @pl.when(inner)
            def _():
                for g in range(2):
                    over(place // 2, g).wait_recv()
                    outward(place, g).start()

    def swap_a(p):
        return remote(send_a.at[p], recv_a.at[p], a_send.at[p], a_recv.at[p], "head", pair)

    def swap_b(p):
        return remote(send_b.at[p], recv_b.at[p], b_send.at[p], b_recv.at[p], "head", across)

    def swap_c(p):
        part = out_ref.at[side, seq_of(p)]
        return remote(part, part, c_send.at[p], c_recv.at[p], "head", pair)

    wide = 2 * LANES

    def project(place):
        attended = jnp.concatenate(
            [
                ag[place, g, h * draft : (h + 1) * draft, :].astype(jnp.bfloat16)
                for g in range(2)
                for h in range(rows // draft)
            ],
            axis=1,
        )
        for target, which in ((send_a, other), (keep, side)):
            @pl.loop(0, half // wide)
            def _(i):
                at = pl.ds(pl.multiple_of(i * wide, wide), wide)
                target[place, :, at] = jnp.dot(
                    attended, wbuf[which, :, at], preferred_element_type=jnp.float32
                )
            if target is send_a:
                swap_a(place).start()

    def join_pair(place):
        swap_a(place).wait_recv()
        send_b[place] = keep[place] + recv_a[place]
        swap_b(place).start()

    def join_across(place):
        swap_b(place).wait_recv()
        out_ref[side, seq_of(place)] = send_b[place] + recv_b[place]
        swap_c(place).start()

    attend(0)
    pl.semaphore_wait(barrier, 4)
    send_inward(0)
    attend(1)
    send_inward(1)
    merge(0)
    attend(2)
    send_inward(2)
    attend(3)
    send_inward(3)
    w_copy(0).wait()
    w_copy(1).wait()
    finish(0)
    arrive(1)
    project(1)
    merge(1)
    arrive(0)
    project(0)
    join_pair(1)
    finish(1)
    arrive(3)
    project(3)
    join_pair(0)
    join_across(1)
    arrive(2)
    project(2)
    join_pair(3)
    join_across(0)
    join_pair(2)
    join_across(3)
    join_across(2)

    for place in range(4):
        swap_c(place).wait_recv()
        swap_a(place).wait_send()
        swap_b(place).wait_send()
        swap_c(place).wait_send()

    @pl.when(outer)
    def _():
        for place in range(4):
            for g in range(2):
                inward(place, g).wait_send()

    @pl.when(inner)
    def _():
        for g in range(2):
            for place in range(4):
                outward(place, g).wait_send()
            for i in range(2):
                through(i, g).wait_send()
                over(i, g).wait_send()


def shards(n, query, key_cache, value_cache, new_key, new_value, lengths, out_weight):
    seqs, q_count, draft, dim = query.shape
    ctx_len, kv_count = key_cache.shape[1:3]
    rows = q_count // 2 * draft
    features, width = out_weight.shape
    span = 2 * ctx_len
    chunk = 8 * PAGE
    half = width // 2
    message = rows + 8 * (rows // LANES)
    f32 = jnp.float32
    vmem = pl.BlockSpec(memory_space=pltpu.VMEM)
    anywhere = pl.BlockSpec(memory_space=pl.ANY)
    dma = pltpu.SemaphoreType.DMA
    out = pl.pallas_call(
        functools.partial(kernel, draft, chunk),
        out_shape=jax.ShapeDtypeStruct((2, seqs, draft, half), f32),
        in_specs=[
            vmem, anywhere, anywhere, vmem, vmem,
            pl.BlockSpec(memory_space=pltpu.SMEM), anywhere,
        ],
        out_specs=vmem,
        scratch_shapes=[
            pltpu.VMEM((n, span, dim), key_cache.dtype),
            pltpu.VMEM((n, span, dim), value_cache.dtype),
            pltpu.VMEM((2, features, half), out_weight.dtype),
            pltpu.VMEM((span // chunk, rows, chunk), f32),
            pltpu.VMEM((rows, 2 * dim), f32),
            pltpu.VMEM((n, 2, message, dim), f32),
            pltpu.VMEM((n, 2, message, dim), f32),
            pltpu.VMEM((n // 2, 2, message, dim), f32),
            pltpu.VMEM((n // 2, 2, message, dim), f32),
            pltpu.VMEM((n, 2, rows, dim), f32),
        ]
        + [pltpu.VMEM((n, draft, half), f32)] * 5
        + [dma((n,)), dma((n,)), dma((2,))]
        + [dma((n, 2))] * 2
        + [dma((n // 2, 2))] * 2
        + [dma((n, 2))] * 2
        + [dma((n // 2, 2))] * 2
        + [dma((n,))] * 6,
        compiler_params=pltpu.CompilerParams(
            collective_id=0, has_side_effects=True, vmem_limit_bytes=56 * 2**20
        ),
    )(
        query.reshape(seqs, q_count * draft, dim),
        key_cache.reshape(seqs, span, dim),
        value_cache.reshape(seqs, span, dim),
        new_key, new_value, lengths, out_weight,
    )
    return jnp.transpose(out, (1, 2, 0, 3)).reshape(seqs, draft, width)


def solution(mesh):
    placed = (
        P("groups", "head", None, None),
        P("groups", "ctx", "head", None),
        P("groups", "ctx", "head", None),
        P("groups", "head", None, None),
        P("groups", "head", None, None),
        P("groups"),
        P("head", "ctx"),
    )
    ctx, heads = mesh.shape["ctx"], mesh.shape["head"]

    def body(query, key_cache, *rest):
        fits = (
            query.shape[0] == ctx
            and ctx == 4
            and heads == 4
            and key_cache.shape[2] == 2
            and query.shape[3] == LANES
            and key_cache.shape[1] % (4 * PAGE) == 0
        )
        if fits:
            return shards(ctx, query, key_cache, *rest)
        return plain_shards(query, key_cache, *rest)

    return jax.shard_map(
        body, mesh=mesh, in_specs=placed, out_specs=P("groups", None, "ctx"), check_vma=False
    )
```

time: 72.3 us -> 59.8 us (0.83)
  Pallas kernels: 69.8 us -> 57.4 us
    pallas_call x1, Pallas kernels: 69.8 us -> 57.4 us  [shards(): pl.pallas_call(functools.partial(kernel, draft, chunk), out_shape=jax.Sha...]
where the time goes in v2:
time: 59.8 us; the launch traced here: 59.7 us
  Pallas kernels  57.4 us (96%)
  local copies, waits for them, and re-layouts  2.31 us (4%)
    pallas_call x1, Pallas kernels, shards(): pl.pallas_call(functools.partial(kernel, draft, chunk), out_shape=jax.Sha...  57.4 us
    reshape x1, local copies, waits for them, and re-layouts, shards(): return jnp.transpose(out, (1, 2, 0, 3)).reshape(seqs, draft, width)  2.31 us

profile of v2, /device:TPU:0, one launch (start us, length us, event | category | flops | bytes accessed | tf_op | source)
XLA Modules:
  0.0 59.7 jit_solution(4121113286062665763)
XLA Ops:
  0.0 57.4 %shard_map.73 = f32[2,4,32,1024]{3,2,1,0:T(8,128)} custom-call(bf16[4,512,128]{2,1,0:T(8,128)(2,1)} %bitcast.9, bf16[4,4096,128]{2,1,0:T(8,128)(2,1)} %bitcast.6, bf16[4,4096,128]{2,1,0:T(8,128)(2,1)} %bitcast.7, bf16[4,2,32,128]{3,2,1,0:T(8,128)(2,1)} %nk_ref.1, bf16[4,2,32,128]{3,2,1,0:T(8,128)(2,1)} %nv_ref.1, s32[4]{0:T(128)} %len_ref.1, ...), custom_call_target="tpu_custom_call" | custom-call | tf_op jit(solution)/shard_map/pallas_call | solution.py:409
  57.4 2.3 %copy.9 = f32[2,4,4,8,1024]{4,3,0,2,1:T(8,128)} copy(f32[2,4,4,8,1024]{4,3,2,1,0:T(8,128)} %bitcast.8) | data formatting | bytes 2097152 | tf_op jit(solution)/shard_map/reshape | solution.py:445

commit v3 on v2

--- a/solution.py
+++ b/solution.py
@@ -291,12 +291,12 @@
             for g in range(2):
                 outward(place, g).wait_recv()
 
-        if place % 2 == 0:
-            @pl.when(inner)
-            def _():
-                for g in range(2):
-                    over(place // 2, g).wait_recv()
-                    outward(place, g).start()
+    def relay(i):
+        @pl.when(inner)
+        def _():
+            for g in range(2):
+                over(i, g).wait_recv()
+                outward(2 * i, g).start()
 
     def swap_a(p):
         return remote(send_a.at[p], recv_a.at[p], a_send.at[p], a_recv.at[p], "head", pair)
@@ -355,18 +355,20 @@
     arrive(1)
     project(1)
     merge(1)
+    relay(0)
+    join_pair(1)
     arrive(0)
     project(0)
-    join_pair(1)
     finish(1)
+    join_pair(0)
+    join_across(1)
     arrive(3)
     project(3)
-    join_pair(0)
-    join_across(1)
+    relay(1)
+    join_pair(3)
+    join_across(0)
     arrive(2)
     project(2)
-    join_pair(3)
-    join_across(0)
     join_pair(2)
     join_across(3)
     join_across(2)

time: 59.8 us -> 58.4 us (0.977)
  Pallas kernels: 57.4 us -> 55.9 us
    pallas_call x1, Pallas kernels: 57.4 us -> 55.9 us  [shards(): pl.pallas_call(functools.partial(kernel, draft, chunk), out_shape=jax.Sha...]
where the time goes in v3:
time: 58.4 us; the launch traced here: 58.3 us
  Pallas kernels  55.9 us (96%)
  local copies, waits for them, and re-layouts  2.31 us (4%)
    pallas_call x1, Pallas kernels, shards(): pl.pallas_call(functools.partial(kernel, draft, chunk), out_shape=jax.Sha...  55.9 us
    reshape x1, local copies, waits for them, and re-layouts, shards(): return jnp.transpose(out, (1, 2, 0, 3)).reshape(seqs, draft, width)  2.31 us

profile of v3, /device:TPU:0, one launch (start us, length us, event | category | flops | bytes accessed | tf_op | source)
XLA Modules:
  0.0 58.3 jit_solution(4637281710216508694)
XLA Ops:
  0.0 55.9 %shard_map.73 = f32[2,4,32,1024]{3,2,1,0:T(8,128)} custom-call(bf16[4,512,128]{2,1,0:T(8,128)(2,1)} %bitcast.9, bf16[4,4096,128]{2,1,0:T(8,128)(2,1)} %bitcast.6, bf16[4,4096,128]{2,1,0:T(8,128)(2,1)} %bitcast.7, bf16[4,2,32,128]{3,2,1,0:T(8,128)(2,1)} %nk_ref.1, bf16[4,2,32,128]{3,2,1,0:T(8,128)(2,1)} %nv_ref.1, s32[4]{0:T(128)} %len_ref.1, ...), custom_call_target="tpu_custom_call" | custom-call | tf_op jit(solution)/shard_map/pallas_call | solution.py:411
  56.0 2.3 %copy.9 = f32[2,4,4,8,1024]{4,3,0,2,1:T(8,128)} copy(f32[2,4,4,8,1024]{4,3,2,1,0:T(8,128)} %bitcast.8) | data formatting | bytes 2097152 | tf_op jit(solution)/shard_map/reshape | solution.py:447
